TPU v7x, 32 devices: a whole 2x2x4 slice. The times are simulated.
32 devices in a mesh: sky: 4 (over x, core), tm: 8 (over z, y).
Axes of the slice: x: 2, y: 2, z: 4, core: 2. Of those that a mesh axis runs over, the one named last changes fastest.
Arguments:
- attitude: float32 [4, 8, 512], P(None, 'tm', 'sky'), may hold values from -6 to 6
- slot_time: float32 [262144], P(('sky', 'tm')), may hold values from -1 to 1
- slot_parallax: float32 [262144], P(('sky', 'tm')), may hold values from -1 to 1
- slot_observed: float32 [262144], P(('sky', 'tm')), may hold values from -6 to 6
- slot_phase: float32 [262144], P(('sky', 'tm')), may hold values from 0 to 1
- slot_knot: int32 [262144], P(('sky', 'tm')), may hold values from 0 to 508
- block_source: int32 [8192], P(('sky', 'tm')), may hold values from 0 to 63
- block_count: int32 [8192], P(('sky', 'tm')), may hold values from 1 to 32
- prior: float32 [5, 256], P(None, ('sky', 'tm')), may hold values from 0.5 to 4
Outputs:
- update: float32 [5, 256], P(None, ('sky', 'tm'))
Inputs may be any that keep to these rules, and one draw needn't show every extreme that they name: The four knots from slot_knot on lie in the transit's time group of 512 knots. `block_source`: an index into the 64 sources of the block's own sky sector.
All inputs are finite; a program needn't handle non-finite values.
Results may differ from a plain program's by a relative error of at most 0.0003.
Values sent between devices are 32-bit elements; how exact they have to be, the bound alone decides.
A program may use at most 64 MiB of HBM per device.

v0:
```python
import math

import jax
import jax.numpy as jnp
from jax import lax
from jax.sharding import PartitionSpec as P

PAIR_LIST = [(i, j) for i in range(5) for j in range(i, 5)]


def spline_quat(table, knot, phase):
    total = knot.shape[0]
    width = table.shape[1]
    step = math.gcd(total, 512)
    knot_rows = knot.reshape(total // step, step)
    phase_rows = phase.reshape(total // step, step)
    positions = jnp.arange(width, dtype=jnp.int32)

    def one_block(items):
        knot_here, phase_here = items
        weights = [
            (1.0 - phase_here) ** 3 / 6.0,
            (3.0 * phase_here**3 - 6.0 * phase_here**2 + 4.0) / 6.0,
            (-3.0 * phase_here**3 + 3.0 * phase_here**2 + 3.0 * phase_here + 1.0) / 6.0,
            phase_here**3 / 6.0,
        ]
        offset = positions[None, :] - knot_here[:, None]
        spread = jnp.zeros((step, width), jnp.float32)
        for i in range(4):
            spread = jnp.where(offset == i, weights[i][:, None], spread)
        return lax.dot_general(
            table,
            spread,
            (((1,), (1,)), ((), ())),
            precision=lax.Precision.HIGHEST,
            preferred_element_type=jnp.float32,
        )

    quat = lax.map(one_block, (knot_rows, phase_rows))
    return jnp.transpose(quat, (1, 0, 2)).reshape(4, total)


def block_sums(table, knot, phase, time, parallax, observed, count):
    quat = spline_quat(table, knot, phase)
    cross = quat[0] * quat[0] + quat[1] * quat[1] - quat[2] * quat[2] - quat[3] * quat[3]
    along = 2.0 * (quat[1] * quat[2] + quat[0] * quat[3])
    tilt = 2.0 * (quat[1] * quat[3] - quat[0] * quat[2])
    design = [cross, along, parallax, time * cross, time * along]
    residual = observed - tilt
    rows = [design[i] * design[j] for i, j in PAIR_LIST] + [design[i] * residual for i in range(5)]
    stacked = jnp.stack(rows)
    blocks = count.shape[0]
    stacked = stacked.reshape(20, blocks, -1)
    live = (jnp.arange(stacked.shape[2], dtype=jnp.int32)[None, :] < count[:, None]).astype(
        stacked.dtype
    )
    return jnp.sum(stacked * live[None], axis=2)


def source_sums(sums, block_source, sector_sources):
    blocks = block_source.shape[0]
    step = math.gcd(blocks, 512)
    source_rows = block_source.reshape(blocks // step, step)
    sum_rows = jnp.transpose(sums.reshape(20, blocks // step, step), (1, 0, 2))
    positions = jnp.arange(sector_sources, dtype=jnp.int32)

    def add_block(carry, items):
        source_here, sums_here = items
        member = (source_here[:, None] == positions[None, :]).astype(jnp.float32)
        return (
            carry
            + jnp.dot(
                sums_here,
                member,
                precision=lax.Precision.HIGHEST,
                preferred_element_type=jnp.float32,
            ),
            None,
        )

    start = jnp.zeros((20, sector_sources), jnp.float32)
    total, _ = lax.scan(add_block, start, (source_rows, sum_rows))
    return total


def solve_normals(normal, prior):
    entry = {}
    for index, pair in enumerate(PAIR_LIST):
        entry[pair[1], pair[0]] = normal[index]
    for i in range(5):
        entry[i, i] = entry[i, i] + prior[i]
    lower = {}
    for col in range(5):
        pivot = entry[col, col]
        for k in range(col):
            pivot = pivot - lower[col, k] * lower[col, k]
        root = jnp.sqrt(pivot)
        lower[col, col] = root
        for row in range(col + 1, 5):
            value = entry[row, col]
            for k in range(col):
                value = value - lower[row, k] * lower[col, k]
            lower[row, col] = value / root
    forward = []
    for i in range(5):
        value = normal[15 + i]
        for k in range(i):
            value = value - lower[i, k] * forward[k]
        forward.append(value / lower[i, i])
    result = [None] * 5
    for i in range(4, -1, -1):
        value = forward[i]
        for k in range(i + 1, 5):
            value = value - lower[k, i] * result[k]
        result[i] = value / lower[i, i]
    return jnp.stack(result)


def on_device(
    attitude,
    slot_time,
    slot_parallax,
    slot_observed,
    slot_phase,
    slot_knot,
    block_source,
    block_count,
    prior,
):
    group = lax.all_gather(attitude, "sky", axis=2, tiled=True)
    table = group[:, 0, :]
    sums = block_sums(
        table, slot_knot, slot_phase, slot_time, slot_parallax, slot_observed, block_count
    )
    owned = prior.shape[1]
    sector_sources = owned * lax.axis_size("tm")
    partial_value = source_sums(sums, block_source, sector_sources)
    total = lax.psum(partial_value, "tm")
    normal = lax.dynamic_slice_in_dim(total, lax.axis_index("tm") * owned, owned, 1)
    return solve_normals(normal, prior)


def solution(mesh):
    in_specs = (
        P(None, "tm", "sky"),
        P(("sky", "tm")),
        P(("sky", "tm")),
        P(("sky", "tm")),
        P(("sky", "tm")),
        P(("sky", "tm")),
        P(("sky", "tm")),
        P(("sky", "tm")),
        P(None, ("sky", "tm")),
    )
    out_specs = P(None, ("sky", "tm"))
    return jax.shard_map(
        on_device, mesh=mesh, in_specs=in_specs, out_specs=out_specs, check_vma=False
    )
```

profile of v0, /device:TPU:0, one launch (start us, length us, event | category | flops | bytes accessed | tf_op | source)
XLA Modules:
  0.0 77.9 jit_solution(18191354367063263991)
XLA Ops:
  0.0 0.8 reshape.292
  0.8 0.7 copy-done.4
  1.5 6.2 %all_gather.3 = f32[4,1,512]{2,0,1:T(4,128)S(1)} all-gather(f32[4,1,128]{2,0,1:T(4,128)S(1)} %bitcast.33), channel_id=1, replica_groups=mesh['sky'=4,'tm'=8] {'sky'}, dimensions={2}, use_global_device_ids=true | all-gather | bytes 10240 | tf_op jit(solution)/shard_map/all_gather | solution.py:130
  7.6 22.9 %while.3 = (s32[]{:T(128)}, f32[16,4,512]{2,1,0:T(4,128)S(1)}, s32[16,512]{1,0:T(8,128)S(1)}, f32[16,512]{1,0:T(8,128)S(1)}, f32[4,512]{1,0:T(4,128)S(1)}, /*index=5*/s32[]{:T(128)}) while((s32[]{:T(128)}, f32[16,4,512]{2,1,0:T(4,128)S(1)}, s32[16,512]{1,0:T(8,128)S(1)}, f32[16,512]{1,0:T(8,128)S(1)}, f32[4,512]{1,0:T(4,128)S(1)}, ...), condition=%wide.region_1.2_spmd.clone, body=%wide.region_0.1_spmd.clone.sunk | while | flops 14951938 | bytes 45145 | solution.py:39
  7.6 1.4 %fusion.59 = f32[16,4,512]{2,1,0:T(4,128)S(1)} fusion(f32[16,4,512]{2,1,0:T(4,128)S(1)} %get-tuple-element.192, s32[]{:T(128)S(6)} %copy.59, f32[4,512]{1,0:T(4,128)S(1)} %get-tuple-element.201, f32[512]{0:T(512)S(1)} %get-tuple-element.181, f32[512]{0:T(512)S(1)} %get-tuple-element.182, f32[512]{0:T(512)S(1)} %get-tuple-element.183, ...), kind=kOutput, calls=%fused_computation.2.clone.1 | convolution fusion | flops 14942208 | bytes 26628 | tf_op jit(solution)/shard_map/while/body/eval_jaxpr/dot_general | solution.py:31
  9.1 1.4 %fusion.59 = f32[16,4,512]{2,1,0:T(4,128)S(1)} fusion(f32[16,4,512]{2,1,0:T(4,128)S(1)} %get-tuple-element.192, s32[]{:T(128)S(6)} %copy.59, f32[4,512]{1,0:T(4,128)S(1)} %get-tuple-element.201, f32[512]{0:T(512)S(1)} %get-tuple-element.181, f32[512]{0:T(512)S(1)} %get-tuple-element.182, f32[512]{0:T(512)S(1)} %get-tuple-element.183, ...), kind=kOutput, calls=%fused_computation.2.clone.1 | convolution fusion | flops 14942208 | bytes 26628 | tf_op jit(solution)/shard_map/while/body/eval_jaxpr/dot_general | solution.py:31
  10.5 1.4 %fusion.59 = f32[16,4,512]{2,1,0:T(4,128)S(1)} fusion(f32[16,4,512]{2,1,0:T(4,128)S(1)} %get-tuple-element.192, s32[]{:T(128)S(6)} %copy.59, f32[4,512]{1,0:T(4,128)S(1)} %get-tuple-element.201, f32[512]{0:T(512)S(1)} %get-tuple-element.181, f32[512]{0:T(512)S(1)} %get-tuple-element.182, f32[512]{0:T(512)S(1)} %get-tuple-element.183, ...), kind=kOutput, calls=%fused_computation.2.clone.1 | convolution fusion | flops 14942208 | bytes 26628 | tf_op jit(solution)/shard_map/while/body/eval_jaxpr/dot_general | solution.py:31
  12.0 1.4 %fusion.59 = f32[16,4,512]{2,1,0:T(4,128)S(1)} fusion(f32[16,4,512]{2,1,0:T(4,128)S(1)} %get-tuple-element.192, s32[]{:T(128)S(6)} %copy.59, f32[4,512]{1,0:T(4,128)S(1)} %get-tuple-element.201, f32[512]{0:T(512)S(1)} %get-tuple-element.181, f32[512]{0:T(512)S(1)} %get-tuple-element.182, f32[512]{0:T(512)S(1)} %get-tuple-element.183, ...), kind=kOutput, calls=%fused_computation.2.clone.1 | convolution fusion | flops 14942208 | bytes 26628 | tf_op jit(solution)/shard_map/while/body/eval_jaxpr/dot_general | solution.py:31
  13.4 1.4 %fusion.59 = f32[16,4,512]{2,1,0:T(4,128)S(1)} fusion(f32[16,4,512]{2,1,0:T(4,128)S(1)} %get-tuple-element.192, s32[]{:T(128)S(6)} %copy.59, f32[4,512]{1,0:T(4,128)S(1)} %get-tuple-element.201, f32[512]{0:T(512)S(1)} %get-tuple-element.181, f32[512]{0:T(512)S(1)} %get-tuple-element.182, f32[512]{0:T(512)S(1)} %get-tuple-element.183, ...), kind=kOutput, calls=%fused_computation.2.clone.1 | convolution fusion | flops 14942208 | bytes 26628 | tf_op jit(solution)/shard_map/while/body/eval_jaxpr/dot_general | solution.py:31
  14.8 1.4 %fusion.59 = f32[16,4,512]{2,1,0:T(4,128)S(1)} fusion(f32[16,4,512]{2,1,0:T(4,128)S(1)} %get-tuple-element.192, s32[]{:T(128)S(6)} %copy.59, f32[4,512]{1,0:T(4,128)S(1)} %get-tuple-element.201, f32[512]{0:T(512)S(1)} %get-tuple-element.181, f32[512]{0:T(512)S(1)} %get-tuple-element.182, f32[512]{0:T(512)S(1)} %get-tuple-element.183, ...), kind=kOutput, calls=%fused_computation.2.clone.1 | convolution fusion | flops 14942208 | bytes 26628 | tf_op jit(solution)/shard_map/while/body/eval_jaxpr/dot_general | solution.py:31
  16.3 1.4 %fusion.59 = f32[16,4,512]{2,1,0:T(4,128)S(1)} fusion(f32[16,4,512]{2,1,0:T(4,128)S(1)} %get-tuple-element.192, s32[]{:T(128)S(6)} %copy.59, f32[4,512]{1,0:T(4,128)S(1)} %get-tuple-element.201, f32[512]{0:T(512)S(1)} %get-tuple-element.181, f32[512]{0:T(512)S(1)} %get-tuple-element.182, f32[512]{0:T(512)S(1)} %get-tuple-element.183, ...), kind=kOutput, calls=%fused_computation.2.clone.1 | convolution fusion | flops 14942208 | bytes 26628 | tf_op jit(solution)/shard_map/while/body/eval_jaxpr/dot_general | solution.py:31
  17.7 1.4 %fusion.59 = f32[16,4,512]{2,1,0:T(4,128)S(1)} fusion(f32[16,4,512]{2,1,0:T(4,128)S(1)} %get-tuple-element.192, s32[]{:T(128)S(6)} %copy.59, f32[4,512]{1,0:T(4,128)S(1)} %get-tuple-element.201, f32[512]{0:T(512)S(1)} %get-tuple-element.181, f32[512]{0:T(512)S(1)} %get-tuple-element.182, f32[512]{0:T(512)S(1)} %get-tuple-element.183, ...), kind=kOutput, calls=%fused_computation.2.clone.1 | convolution fusion | flops 14942208 | bytes 26628 | tf_op jit(solution)/shard_map/while/body/eval_jaxpr/dot_general | solution.py:31
  19.1 1.4 %fusion.59 = f32[16,4,512]{2,1,0:T(4,128)S(1)} fusion(f32[16,4,512]{2,1,0:T(4,128)S(1)} %get-tuple-element.192, s32[]{:T(128)S(6)} %copy.59, f32[4,512]{1,0:T(4,128)S(1)} %get-tuple-element.201, f32[512]{0:T(512)S(1)} %get-tuple-element.181, f32[512]{0:T(512)S(1)} %get-tuple-element.182, f32[512]{0:T(512)S(1)} %get-tuple-element.183, ...), kind=kOutput, calls=%fused_computation.2.clone.1 | convolution fusion | flops 14942208 | bytes 26628 | tf_op jit(solution)/shard_map/while/body/eval_jaxpr/dot_general | solution.py:31
  20.6 1.4 %fusion.59 = f32[16,4,512]{2,1,0:T(4,128)S(1)} fusion(f32[16,4,512]{2,1,0:T(4,128)S(1)} %get-tuple-element.192, s32[]{:T(128)S(6)} %copy.59, f32[4,512]{1,0:T(4,128)S(1)} %get-tuple-element.201, f32[512]{0:T(512)S(1)} %get-tuple-element.181, f32[512]{0:T(512)S(1)} %get-tuple-element.182, f32[512]{0:T(512)S(1)} %get-tuple-element.183, ...), kind=kOutput, calls=%fused_computation.2.clone.1 | convolution fusion | flops 14942208 | bytes 26628 | tf_op jit(solution)/shard_map/while/body/eval_jaxpr/dot_general | solution.py:31
  22.0 1.4 %fusion.59 = f32[16,4,512]{2,1,0:T(4,128)S(1)} fusion(f32[16,4,512]{2,1,0:T(4,128)S(1)} %get-tuple-element.192, s32[]{:T(128)S(6)} %copy.59, f32[4,512]{1,0:T(4,128)S(1)} %get-tuple-element.201, f32[512]{0:T(512)S(1)} %get-tuple-element.181, f32[512]{0:T(512)S(1)} %get-tuple-element.182, f32[512]{0:T(512)S(1)} %get-tuple-element.183, ...), kind=kOutput, calls=%fused_computation.2.clone.1 | convolution fusion | flops 14942208 | bytes 26628 | tf_op jit(solution)/shard_map/while/body/eval_jaxpr/dot_general | solution.py:31
  23.4 1.4 %fusion.59 = f32[16,4,512]{2,1,0:T(4,128)S(1)} fusion(f32[16,4,512]{2,1,0:T(4,128)S(1)} %get-tuple-element.192, s32[]{:T(128)S(6)} %copy.59, f32[4,512]{1,0:T(4,128)S(1)} %get-tuple-element.201, f32[512]{0:T(512)S(1)} %get-tuple-element.181, f32[512]{0:T(512)S(1)} %get-tuple-element.182, f32[512]{0:T(512)S(1)} %get-tuple-element.183, ...), kind=kOutput, calls=%fused_computation.2.clone.1 | convolution fusion | flops 14942208 | bytes 26628 | tf_op jit(solution)/shard_map/while/body/eval_jaxpr/dot_general | solution.py:31
  24.9 1.4 %fusion.59 = f32[16,4,512]{2,1,0:T(4,128)S(1)} fusion(f32[16,4,512]{2,1,0:T(4,128)S(1)} %get-tuple-element.192, s32[]{:T(128)S(6)} %copy.59, f32[4,512]{1,0:T(4,128)S(1)} %get-tuple-element.201, f32[512]{0:T(512)S(1)} %get-tuple-element.181, f32[512]{0:T(512)S(1)} %get-tuple-element.182, f32[512]{0:T(512)S(1)} %get-tuple-element.183, ...), kind=kOutput, calls=%fused_computation.2.clone.1 | convolution fusion | flops 14942208 | bytes 26628 | tf_op jit(solution)/shard_map/while/body/eval_jaxpr/dot_general | solution.py:31
  26.3 1.4 %fusion.59 = f32[16,4,512]{2,1,0:T(4,128)S(1)} fusion(f32[16,4,512]{2,1,0:T(4,128)S(1)} %get-tuple-element.192, s32[]{:T(128)S(6)} %copy.59, f32[4,512]{1,0:T(4,128)S(1)} %get-tuple-element.201, f32[512]{0:T(512)S(1)} %get-tuple-element.181, f32[512]{0:T(512)S(1)} %get-tuple-element.182, f32[512]{0:T(512)S(1)} %get-tuple-element.183, ...), kind=kOutput, calls=%fused_computation.2.clone.1 | convolution fusion | flops 14942208 | bytes 26628 | tf_op jit(solution)/shard_map/while/body/eval_jaxpr/dot_general | solution.py:31
  27.7 1.4 %fusion.59 = f32[16,4,512]{2,1,0:T(4,128)S(1)} fusion(f32[16,4,512]{2,1,0:T(4,128)S(1)} %get-tuple-element.192, s32[]{:T(128)S(6)} %copy.59, f32[4,512]{1,0:T(4,128)S(1)} %get-tuple-element.201, f32[512]{0:T(512)S(1)} %get-tuple-element.181, f32[512]{0:T(512)S(1)} %get-tuple-element.182, f32[512]{0:T(512)S(1)} %get-tuple-element.183, ...), kind=kOutput, calls=%fused_computation.2.clone.1 | convolution fusion | flops 14942208 | bytes 26628 | tf_op jit(solution)/shard_map/while/body/eval_jaxpr/dot_general | solution.py:31
  29.2 1.4 %fusion.59 = f32[16,4,512]{2,1,0:T(4,128)S(1)} fusion(f32[16,4,512]{2,1,0:T(4,128)S(1)} %get-tuple-element.192, s32[]{:T(128)S(6)} %copy.59, f32[4,512]{1,0:T(4,128)S(1)} %get-tuple-element.201, f32[512]{0:T(512)S(1)} %get-tuple-element.181, f32[512]{0:T(512)S(1)} %get-tuple-element.182, f32[512]{0:T(512)S(1)} %get-tuple-element.183, ...), kind=kOutput, calls=%fused_computation.2.clone.1 | convolution fusion | flops 14942208 | bytes 26628 | tf_op jit(solution)/shard_map/while/body/eval_jaxpr/dot_general | solution.py:31
  30.5 0.4 multiply_reduce_fusion.1
  31.0 0.1 reshape.294
  31.2 0.1 reshape.295
  31.3 0.7 copy-done
  32.1 0.7 copy-done.1
  32.9 0.1 stack.65
  33.0 0.1 copy.27
  33.1 0.1 stack.66
  33.2 0.1 copy.28
  33.3 0.1 stack.67
  33.4 0.1 copy.29
  33.5 0.1 reshape.296
  33.6 0.1 stack.68
  33.7 0.1 copy.31
  33.8 0.1 stack.69
  33.9 0.1 copy.32
  34.0 0.1 stack.70
  34.2 0.1 stack.71
  34.4 0.1 stack.72
  34.5 0.1 stack.73
  34.7 0.1 stack.74
  34.9 0.1 stack.75
  35.1 0.1 stack.76
  35.3 0.1 stack.77
  35.4 0.1 stack.78
  35.6 0.1 stack.79
  35.8 0.1 stack.80
  36.0 0.1 stack.81
  36.2 0.7 copy-done.6
  36.8 0.1 multiply_reduce_fusion
  36.9 0.6 copy-done.7
  37.5 0.3 fusion.39
  37.9 37.9 %psum.7 = f32[20,64]{0,1:T(8,128)S(1)} all-reduce(f32[20,64]{0,1:T(8,128)S(1)} %fusion.39), channel_id=1, replica_groups=mesh['sky'=4,'tm'=8] {'tm'}, use_global_device_ids=true, to_apply=%region_3.4 | all-reduce | flops 1280 | bytes 10240 | tf_op jit(solution)/shard_map/psum | solution.py:138
  75.8 0.7 copy-done.5
  76.5 0.1 copy.54
  76.5 0.1 copy.53
  76.6 0.1 copy.52
  76.7 0.1 copy.51
  76.8 0.1 subtract_divide_fusion.7
  76.9 0.1 subtract_divide_fusion.4
  77.0 0.1 copy.55
  77.1 0.1 subtract_divide_fusion
  77.2 0.1 stack.83
  77.3 0.7 copy.50
  (101 shorter events, 2.0 us)
Async XLA Ops:
  0.0 0.8 copy-start.3
  0.8 0.7 copy-start.4
  31.3 0.8 copy-start
  31.3 0.8 %copy-start.2 = (f32[8192]{0:T(1024)S(1)}, f32[8192]{0:T(1024)}, u32[]{:S(2)}) copy-start(f32[8192]{0:T(1024)} %param.14) | copy-start | bytes 98308
  32.1 0.8 copy-start.1
  36.1 0.7 copy-start.6
  36.8 0.7 copy-start.7
  75.8 0.7 copy-start.5
where the time goes:
time: 78.4 us; the launch traced here: 77.9 us
  blocking collectives  44.1 us (56%)
  matrix products  22.3 us (28%)
  local copies, waits for them, and re-layouts  9.75 us (12%)
  other arithmetic  1.07 us (1%)
    psum x1, blocking collectives, on_device(): total = lax.psum(partial_value, 'tm')  37.9 us
    dot_general x16, matrix products, one_block(): lax.dot_general(table, spread, (((1,), (1,)), ((), ())), precision=lax.Pr...  22 us
    all_gather x1, blocking collectives, on_device(): group = lax.all_gather(attitude, 'sky', axis=2, tiled=True)  6.15 us
    unnamed x40, local copies, waits for them, and re-layouts  4.73 us
    another operation x35, local copies, waits for them, and re-layouts, block_sums(): stacked = jnp.stack(rows)  2.6 us

commit v1 on v0

v1 whole, which is shorter than its diff:
```python
import functools

import jax
import jax.numpy as jnp
from jax import lax
from jax.experimental import pallas as pl
from jax.experimental.pallas import tpu as pltpu
from jax.sharding import PartitionSpec as P

PAIR_LIST = [(i, j) for i in range(5) for j in range(i, 5)]
MESH = pl.DeviceIdType.MESH
LANES = 128
ROWS = 32


def lane_gather(row, index):
    wide = jnp.broadcast_to(row, index.shape)
    return jnp.take_along_axis(wide, index, axis=1, mode="promise_in_bounds")


def split3(value):
    high = value.astype(jnp.bfloat16)
    rest = value - high.astype(jnp.float32)
    mid = rest.astype(jnp.bfloat16)
    low = (rest - mid.astype(jnp.float32)).astype(jnp.bfloat16)
    return high, mid, low


def solve_rows(row, prior_row):
    entry = {}
    for index, (i, j) in enumerate(PAIR_LIST):
        entry[j, i] = row(index)
    for i in range(5):
        entry[i, i] = entry[i, i] + prior_row(i)
    right = [row(15 + i) for i in range(5)]
    unit, inverse = {}, []
    for col in range(5):
        inv = 1.0 / entry[col, col]
        inverse.append(inv)
        for r in range(col + 1, 5):
            unit[r, col] = entry[r, col] * inv
        for r in range(col + 1, 5):
            for c in range(col + 1, r + 1):
                entry[r, c] = entry[r, c] - unit[r, col] * entry[c, col]
            right[r] = right[r] - unit[r, col] * right[col]
    result = [right[i] * inverse[i] for i in range(5)]
    for i in range(4, 0, -1):
        for k in range(i):
            result[k] = result[k] - unit[i, k] * result[i]
    return result


def kernel(
    n_sky, n_tm, span,
    attitude_hbm, time_hbm, parallax_hbm, observed_hbm, phase_hbm, knot_hbm,
    source_hbm, count_hbm, prior_hbm,
    out_ref,
    table, coef, time_v, parallax_v, observed_v, phase_v, knot_v, source_v, count_v, prior_v,
    spread, parts, member, tiles, landed, turned,
    local_sem, own_sem, att_send, att_recv, sum_send, sum_recv,
):
    sky = lax.axis_index("sky")
    tm = lax.axis_index("tm")
    rows = time_v.shape[0]
    owned = prior_v.shape[1]
    sources = owned * n_tm
    segs = LANES // span

    barrier = pltpu.get_barrier_semaphore()
    for d in range(1, n_sky):
        pl.semaphore_signal(
            barrier, inc=1, device_id={"sky": lax.rem(sky + d, n_sky)}, device_id_type=MESH
        )
    for d in range(1, n_tm):
        pl.semaphore_signal(
            barrier, inc=1, device_id={"tm": lax.rem(tm + d, n_tm)}, device_id_type=MESH
        )
    own = pltpu.make_async_copy(attitude_hbm, table.at[sky], own_sem)
    own.start()
    locals_ = []
    pairs = (
        (count_hbm, count_v), (source_hbm, source_v), (knot_hbm, knot_v), (phase_hbm, phase_v),
        (time_hbm, time_v), (parallax_hbm, parallax_v), (observed_hbm, observed_v),
        (prior_hbm, prior_v),
    )
    for i, (src, dst) in enumerate(pairs):
        copy = pltpu.make_async_copy(src, dst, local_sem.at[i])
        copy.start()
        locals_.append(copy)

    lane_out = lax.broadcasted_iota(jnp.int32, (LANES, LANES), 1)
    lane_in = lax.broadcasted_iota(jnp.int32, (LANES, LANES), 0)
    base = lane_out - (lane_in // span) * ROWS
    for x in range(20):
        spread[x * LANES : (x + 1) * LANES, :] = jnp.where(base == x, 1.0, 0.0).astype(jnp.bfloat16)

    pl.semaphore_wait(barrier, n_sky - 1 + n_tm - 1)

    sends = []
    for d in range(1, n_sky):
        copy = pltpu.make_async_remote_copy(
            src_ref=attitude_hbm,
            dst_ref=table.at[sky],
            send_sem=att_send.at[d - 1],
            recv_sem=att_recv.at[d - 1],
            device_id={"sky": lax.rem(sky + d, n_sky)},
            device_id_type=MESH,
        )
        copy.start()
        sends.append(copy)

    for copy in locals_:
        copy.wait()

    width = 3 * rows
    lane = lax.broadcasted_iota(jnp.int32, (8, LANES), 1)
    sub = lax.broadcasted_iota(jnp.int32, (8, LANES), 0)
    id_list = []
    for start in range(0, width, LANES):
        block = ((lane + start) % rows) * segs + sub % segs
        got = lane_gather(source_v[0:1, :], block % LANES)
        for c in range(1, source_v.shape[0]):
            got = jnp.where(block // LANES == c, lane_gather(source_v[c : c + 1, :], block % LANES), got)
        id_list.append(got)
    ids = jnp.concatenate(id_list, axis=1)[:, :width]
    which = lax.broadcasted_iota(jnp.int32, (sources, width), 0)
    for q in range(segs):
        hit = jnp.broadcast_to(ids[q : q + 1, :], (sources, width)) == which
        member[q * sources : (q + 1) * sources, :] = jnp.where(hit, 1.0, 0.0).astype(jnp.bfloat16)

    own.wait()
    for d in range(1, n_sky):
        pltpu.make_async_remote_copy(
            src_ref=attitude_hbm,
            dst_ref=table.at[lax.rem(sky + n_sky - d, n_sky)],
            send_sem=att_send.at[d - 1],
            recv_sem=att_recv.at[d - 1],
            device_id={"sky": lax.rem(sky + d, n_sky)},
            device_id_type=MESH,
        ).wait_recv()

    per = table.shape[2] // LANES
    chunks = [
        table[c // per, :, (c % per) * LANES : (c % per + 1) * LANES] for c in range(n_sky * per)
    ]
    n_chunks = len(chunks)
    here = jnp.concatenate(chunks, axis=0)
    after = jnp.concatenate(chunks[1:] + chunks[-1:], axis=0)
    wide_lane = lax.broadcasted_iota(jnp.int32, here.shape, 1)
    a = [here]
    for i in range(1, 4):
        a.append(
            jnp.where(
                wide_lane < LANES - i,
                pltpu.roll(here, LANES - i, 1),
                pltpu.roll(after, LANES - i, 1),
            )
        )
    coef[0] = (a[0] + 4.0 * a[1] + a[2]) * (1.0 / 6.0)
    coef[1] = (a[2] - a[0]) * 0.5
    coef[2] = (a[0] - 2.0 * a[1] + a[2]) * 0.5
    coef[3] = ((a[3] - a[0]) + 3.0 * (a[1] - a[2])) * (1.0 / 6.0)

    def sums_of(v):
        at = slice(v * 8, v * 8 + 8)
        knot = knot_v[at, :]
        u = phase_v[at, :]
        time = time_v[at, :]
        block = (sub + v * 8) * segs + lane // span
        chunk = (v * 8 * segs) // LANES
        count = lane_gather(count_v[chunk : chunk + 1, :], block - chunk * LANES)
        live = lane % span < count
        low, high = knot % LANES, knot // LANES
        picks = [high == c for c in range(n_chunks)]
        quat = []
        for m in range(4):
            value = None
            for j in (3, 2, 1, 0):
                got = lane_gather(coef[j, m : m + 1, :], low)
                for c in range(1, n_chunks):
                    x = c * 4 + m
                    got = jnp.where(picks[c], lane_gather(coef[j, x : x + 1, :], low), got)
                value = got if value is None else value * u + got
            quat.append(value)
        q0, q1, q2, q3 = quat
        cross = jnp.where(live, q0 * q0 + q1 * q1 - q2 * q2 - q3 * q3, 0.0)
        along = jnp.where(live, 2.0 * (q1 * q2 + q0 * q3), 0.0)
        tilt = 2.0 * (q1 * q3 - q0 * q2)
        parallax = jnp.where(live, parallax_v[at, :], 0.0)
        design = [cross, along, parallax, time * cross, time * along]
        residual = observed_v[at, :] - tilt
        return [design[i] * design[j] for i, j in PAIR_LIST] + [d * residual for d in design]

    for v in range(0, rows // 8, 2):
        first, second = sums_of(v), sums_of(v + 1)
        for x in range(20):
            for k, part in enumerate(split3(jnp.concatenate([first[x], second[x]], axis=0))):
                parts[k * rows + v * 8 : k * rows + v * 8 + 16, x * LANES : (x + 1) * LANES] = part

    three = jnp.dot(parts[...], spread[...], preferred_element_type=jnp.float32)
    block_sum = three[:rows] + three[rows : 2 * rows] + three[2 * rows :]
    stacked = jnp.concatenate(split3(block_sum), axis=0)
    by_seg = jnp.dot(member[...], stacked, preferred_element_type=jnp.float32)
    lane_s = lax.broadcasted_iota(jnp.int32, (sources, LANES), 1) // ROWS
    normal = jnp.where(lane_s == 0, by_seg[:sources], 0.0)
    for q in range(1, segs):
        normal = jnp.where(lane_s == q, by_seg[q * sources : (q + 1) * sources], normal)
    tiles[...] = normal.reshape(n_tm, owned, LANES)

    for d in range(1, n_tm):
        peer = lax.rem(tm + d, n_tm)
        copy = pltpu.make_async_remote_copy(
            src_ref=tiles.at[peer],
            dst_ref=landed.at[d - 1],
            send_sem=sum_send.at[d - 1],
            recv_sem=sum_recv.at[d - 1],
            device_id={"tm": peer},
            device_id_type=MESH,
        )
        copy.start()
        sends.append(copy)
    total = tiles[tm]
    for copy in sends[n_sky - 1 :]:
        copy.wait_recv()
    for d in range(1, n_tm):
        total = total + landed[d - 1]
    for shift in range(1, segs):
        pass
    full = total
    for q in range(1, segs):
        full = full + pltpu.roll(total, q * ROWS, 1)
    turned[...] = jnp.transpose(full)
    result = solve_rows(lambda i: turned[i : i + 1, :], lambda i: prior_v[i : i + 1, :])
    for i in range(5):
        out_ref[i : i + 1, :] = result[i]
    for copy in sends:
        copy.wait_send()


def on_device(n_sky, n_tm, attitude, time, parallax, observed, phase, knot, source, count, prior):
    slots, blocks, owned = time.shape[0], source.shape[0], prior.shape[1]
    knots = attitude.shape[2]
    rows = slots // LANES
    span = slots // blocks
    sources = owned * n_tm
    segs = LANES // span
    n_chunks = n_sky * knots // LANES
    shape = (rows, LANES)
    vmem = pltpu.VMEM
    f32, i32, bf16 = jnp.float32, jnp.int32, jnp.bfloat16
    return pl.pallas_call(
        functools.partial(kernel, n_sky, n_tm, span),
        out_shape=jax.ShapeDtypeStruct(prior.shape, f32),
        in_specs=[pl.BlockSpec(memory_space=pl.ANY)] * 9,
        out_specs=pl.BlockSpec(memory_space=pltpu.VMEM),
        scratch_shapes=[
            vmem((n_sky, 4, knots), f32),
            vmem((4, n_chunks * 4, LANES), f32),
            vmem(shape, f32),
            vmem(shape, f32),
            vmem(shape, f32),
            vmem(shape, f32),
            vmem(shape, i32),
            vmem((blocks // LANES, LANES), i32),
            vmem((blocks // LANES, LANES), i32),
            vmem(prior.shape, f32),
            vmem((20 * LANES, LANES), bf16),
            vmem((3 * rows, 20 * LANES), bf16),
            vmem((segs * sources, 3 * rows), bf16),
            vmem((n_tm, owned, LANES), f32),
            vmem((n_tm - 1, owned, LANES), f32),
            vmem((LANES, owned), f32),
            pltpu.SemaphoreType.DMA((8,)),
            pltpu.SemaphoreType.DMA,
            pltpu.SemaphoreType.DMA((n_sky - 1,)),
            pltpu.SemaphoreType.DMA((n_sky - 1,)),
            pltpu.SemaphoreType.DMA((n_tm - 1,)),
            pltpu.SemaphoreType.DMA((n_tm - 1,)),
        ],
        compiler_params=pltpu.CompilerParams(collective_id=0, has_side_effects=True),
    )(
        attitude.reshape(4, knots),
        time.reshape(shape),
        parallax.reshape(shape),
        observed.reshape(shape),
        phase.reshape(shape),
        knot.reshape(shape),
        source.reshape(blocks // LANES, LANES),
        count.reshape(blocks // LANES, LANES),
        prior,
    )


def solution(mesh):
    slot = P(("sky", "tm"))
    in_specs = (P(None, "tm", "sky"),) + (slot,) * 7 + (P(None, ("sky", "tm")),)
    return jax.shard_map(
        functools.partial(on_device, mesh.shape["sky"], mesh.shape["tm"]),
        mesh=mesh,
        in_specs=in_specs,
        out_specs=P(None, ("sky", "tm")),
        check_vma=False,
    )
```

time: 78.4 us -> 15.8 us (0.20)
  blocking collectives: 44.1 us -> 0 us
  matrix products: 22.3 us -> 0 us
  Pallas kernels: 0 us -> 14.3 us
  local copies, waits for them, and re-layouts: 9.75 us -> 1.28 us
  other arithmetic: 1.07 us -> 0 us
    psum x1 -> x0, blocking collectives: 37.9 us -> none  [on_device(): total = lax.psum(partial_value, 'tm')]
    dot_general x17 -> x0, matrix products: 22.3 us -> none  [the longest x16 22 us: one_block(): lax.dot_general(table, spread, (((1,), (1,)), ((), ())), precision=lax.Pr...]
    pallas_call x0 -> x1, Pallas kernels: none -> 14.3 us  [on_device(): pl.pallas_call(functools.partial(kernel, n_sky, n_tm, span), out_shape=ja...]
    all_gather x1 -> x0, blocking collectives: 6.15 us -> none  [on_device(): group = lax.all_gather(attitude, 'sky', axis=2, tiled=True)]
    unnamed x40 -> x1, local copies, waits for them, and re-layouts: 4.73 us -> 1.28 us
    another operation x37 -> x0, local copies, waits for them, and re-layouts: 3.35 us -> none  [the longest x35 2.6 us: block_sums(): stacked = jnp.stack(rows)]
where the time goes in v1:
time: 15.8 us; the launch traced here: 15.6 us
  Pallas kernels  14.3 us (91%)
  local copies, waits for them, and re-layouts  1.28 us (8%)
    pallas_call x1, Pallas kernels, on_device(): pl.pallas_call(functools.partial(kernel, n_sky, n_tm, span), out_shape=ja...  14.3 us
    unnamed x1, local copies, waits for them, and re-layouts  1.28 us

profile of v1, /device:TPU:0, one launch (start us, length us, event | category | flops | bytes accessed | tf_op | source)
XLA Modules:
  0.0 15.6 jit_solution(10530796275877223550)
XLA Ops:
  0.0 14.3 %shard_map.91 = f32[5,8]{1,0:T(8,128)} custom-call(f32[4,128]{1,0:T(4,128)} %bitcast.13, f32[64,128]{1,0:T(8,128)} %bitcast.8, f32[64,128]{1,0:T(8,128)} %bitcast.9, f32[64,128]{1,0:T(8,128)} %bitcast.10, f32[64,128]{1,0:T(8,128)} %bitcast.11, s32[64,128]{1,0:T(8,128)} %bitcast.12, s32[2,128]{1,0:T(2,128)} %bitcast.14, s32[2,128]{1,0:T(2,128)} %bitcast.15, ...), custom_call_target="tpu_custom_call" | custom-call | tf_op jit(solution)/shard_map/pallas_call | solution.py:251
  14.3 1.3 %copy.11 = f32[5,8]{1,0:T(8,128)} copy(f32[5,8]{1,0:T(8,128)} %shard_map.91) | data formatting | bytes 320

commit v2 on v1

--- a/solution.py
+++ b/solution.py
@@ -53,16 +53,20 @@
 def kernel(
     n_sky, n_tm, span,
     attitude_hbm, time_hbm, parallax_hbm, observed_hbm, phase_hbm, knot_hbm,
-    source_hbm, count_hbm, prior_hbm,
+    source_hbm, count_hbm,
     out_ref,
-    table, coef, time_v, parallax_v, observed_v, phase_v, knot_v, source_v, count_v, prior_v,
-    spread, parts, member, tiles, landed, turned,
-    local_sem, own_sem, att_send, att_recv, sum_send, sum_recv,
+    table, coef, reals, ints, spread, parts, member, tiles, landed,
+    real_sem, int_sem, att_send, att_recv, sum_send, sum_recv,
 ):
     sky = lax.axis_index("sky")
     tm = lax.axis_index("tm")
-    rows = time_v.shape[0]
-    owned = prior_v.shape[1]
+    rows = time_hbm.shape[0]
+    owned = tiles.shape[1]
+    wide = source_hbm.shape[0]
+    phase_v, time_v, parallax_v, observed_v = (reals.at[i] for i in range(4))
+    knot_v = ints.at[:rows]
+    source_v = ints.at[rows : rows + wide]
+    count_v = ints.at[rows + wide :]
     sources = owned * n_tm
     segs = LANES // span
 
@@ -75,18 +79,11 @@
         pl.semaphore_signal(
             barrier, inc=1, device_id={"tm": lax.rem(tm + d, n_tm)}, device_id_type=MESH
         )
-    own = pltpu.make_async_copy(attitude_hbm, table.at[sky], own_sem)
-    own.start()
-    locals_ = []
-    pairs = (
-        (count_hbm, count_v), (source_hbm, source_v), (knot_hbm, knot_v), (phase_hbm, phase_v),
-        (time_hbm, time_v), (parallax_hbm, parallax_v), (observed_hbm, observed_v),
-        (prior_hbm, prior_v),
-    )
-    for i, (src, dst) in enumerate(pairs):
-        copy = pltpu.make_async_copy(src, dst, local_sem.at[i])
-        copy.start()
-        locals_.append(copy)
+    pltpu.make_async_copy(attitude_hbm, table.at[sky], att_recv).start()
+    for src, dst in ((source_hbm, source_v), (count_hbm, count_v), (knot_hbm, knot_v)):
+        pltpu.make_async_copy(src, dst, int_sem).start()
+    for i, src in enumerate((phase_hbm, time_hbm, parallax_hbm, observed_hbm)):
+        pltpu.make_async_copy(src, reals.at[i], real_sem).start()
 
     lane_out = lax.broadcasted_iota(jnp.int32, (LANES, LANES), 1)
     lane_in = lax.broadcasted_iota(jnp.int32, (LANES, LANES), 0)
@@ -96,21 +93,17 @@
 
     pl.semaphore_wait(barrier, n_sky - 1 + n_tm - 1)
 
-    sends = []
     for d in range(1, n_sky):
-        copy = pltpu.make_async_remote_copy(
+        pltpu.make_async_remote_copy(
             src_ref=attitude_hbm,
             dst_ref=table.at[sky],
-            send_sem=att_send.at[d - 1],
-            recv_sem=att_recv.at[d - 1],
+            send_sem=att_send,
+            recv_sem=att_recv,
             device_id={"sky": lax.rem(sky + d, n_sky)},
             device_id_type=MESH,
-        )
-        copy.start()
-        sends.append(copy)
-
-    for copy in locals_:
-        copy.wait()
+        ).start()
+
+    pltpu.make_async_copy(ints, ints, int_sem).wait()
 
     width = 3 * rows
     lane = lax.broadcasted_iota(jnp.int32, (8, LANES), 1)
@@ -128,16 +121,8 @@
         hit = jnp.broadcast_to(ids[q : q + 1, :], (sources, width)) == which
         member[q * sources : (q + 1) * sources, :] = jnp.where(hit, 1.0, 0.0).astype(jnp.bfloat16)
 
-    own.wait()
-    for d in range(1, n_sky):
-        pltpu.make_async_remote_copy(
-            src_ref=attitude_hbm,
-            dst_ref=table.at[lax.rem(sky + n_sky - d, n_sky)],
-            send_sem=att_send.at[d - 1],
-            recv_sem=att_recv.at[d - 1],
-            device_id={"sky": lax.rem(sky + d, n_sky)},
-            device_id_type=MESH,
-        ).wait_recv()
+    pltpu.make_async_copy(reals, reals, real_sem).wait()
+    pltpu.make_async_copy(table, table, att_recv).wait()
 
     per = table.shape[2] // LANES
     chunks = [
@@ -209,32 +194,36 @@
 
     for d in range(1, n_tm):
         peer = lax.rem(tm + d, n_tm)
-        copy = pltpu.make_async_remote_copy(
+        pltpu.make_async_remote_copy(
             src_ref=tiles.at[peer],
             dst_ref=landed.at[d - 1],
-            send_sem=sum_send.at[d - 1],
-            recv_sem=sum_recv.at[d - 1],
+            send_sem=sum_send,
+            recv_sem=sum_recv,
             device_id={"tm": peer},
             device_id_type=MESH,
-        )
-        copy.start()
-        sends.append(copy)
+        ).start()
     total = tiles[tm]
-    for copy in sends[n_sky - 1 :]:
-        copy.wait_recv()
+    pltpu.make_async_copy(landed, landed, sum_recv).wait()
     for d in range(1, n_tm):
         total = total + landed[d - 1]
-    for shift in range(1, segs):
-        pass
+    out_ref[...] = total
+    others = table.at[: n_sky - 1]
+    pltpu.make_async_copy(others, others, att_send).wait()
+    pltpu.make_async_copy(landed, landed, sum_send).wait()
+
+
+def solve_kernel(total_ref, prior_hbm, out_ref, turned, prior_ref, sem):
+    copy = pltpu.make_async_copy(prior_hbm, prior_ref, sem)
+    copy.start()
+    total = total_ref[...]
     full = total
-    for q in range(1, segs):
-        full = full + pltpu.roll(total, q * ROWS, 1)
+    for shift in range(ROWS, LANES, ROWS):
+        full = full + pltpu.roll(total, shift, 1)
     turned[...] = jnp.transpose(full)
-    result = solve_rows(lambda i: turned[i : i + 1, :], lambda i: prior_v[i : i + 1, :])
+    copy.wait()
+    result = solve_rows(lambda i: turned[i : i + 1, :], lambda i: prior_ref[i : i + 1, :])
     for i in range(5):
         out_ref[i : i + 1, :] = result[i]
-    for copy in sends:
-        copy.wait_send()
 
 
 def on_device(n_sky, n_tm, attitude, time, parallax, observed, phase, knot, source, count, prior):
@@ -248,35 +237,23 @@
     shape = (rows, LANES)
     vmem = pltpu.VMEM
     f32, i32, bf16 = jnp.float32, jnp.int32, jnp.bfloat16
-    return pl.pallas_call(
+    total = pl.pallas_call(
         functools.partial(kernel, n_sky, n_tm, span),
-        out_shape=jax.ShapeDtypeStruct(prior.shape, f32),
-        in_specs=[pl.BlockSpec(memory_space=pl.ANY)] * 9,
+        out_shape=pltpu.VMEM((owned, LANES), f32),
+        in_specs=[pl.BlockSpec(memory_space=pl.ANY)] * 8,
         out_specs=pl.BlockSpec(memory_space=pltpu.VMEM),
         scratch_shapes=[
             vmem((n_sky, 4, knots), f32),
             vmem((4, n_chunks * 4, LANES), f32),
-            vmem(shape, f32),
-            vmem(shape, f32),
-            vmem(shape, f32),
-            vmem(shape, f32),
-            vmem(shape, i32),
-            vmem((blocks // LANES, LANES), i32),
-            vmem((blocks // LANES, LANES), i32),
-            vmem(prior.shape, f32),
+            vmem((4,) + shape, f32),
+            vmem((rows + 2 * (blocks // LANES), LANES), i32),
             vmem((20 * LANES, LANES), bf16),
             vmem((3 * rows, 20 * LANES), bf16),
             vmem((segs * sources, 3 * rows), bf16),
             vmem((n_tm, owned, LANES), f32),
             vmem((n_tm - 1, owned, LANES), f32),
-            vmem((LANES, owned), f32),
-            pltpu.SemaphoreType.DMA((8,)),
-            pltpu.SemaphoreType.DMA,
-            pltpu.SemaphoreType.DMA((n_sky - 1,)),
-            pltpu.SemaphoreType.DMA((n_sky - 1,)),
-            pltpu.SemaphoreType.DMA((n_tm - 1,)),
-            pltpu.SemaphoreType.DMA((n_tm - 1,)),
-        ],
+        ]
+        + [pltpu.SemaphoreType.DMA] * 6,
         compiler_params=pltpu.CompilerParams(collective_id=0, has_side_effects=True),
     )(
         attitude.reshape(4, knots),
@@ -287,8 +264,13 @@
         knot.reshape(shape),
         source.reshape(blocks // LANES, LANES),
         count.reshape(blocks // LANES, LANES),
-        prior,
     )
+    return pl.pallas_call(
+        solve_kernel,
+        out_shape=jax.ShapeDtypeStruct(prior.shape, f32),
+        in_specs=[pl.BlockSpec(memory_space=pltpu.VMEM), pl.BlockSpec(memory_space=pl.ANY)],
+        scratch_shapes=[vmem((LANES, owned), f32), vmem(prior.shape, f32), pltpu.SemaphoreType.DMA],
+    )(pltpu.with_memory_space_constraint(total, pltpu.VMEM), prior)
 
 
 def solution(mesh):

time: 15.8 us -> 14.8 us (0.937)
  local copies, waits for them, and re-layouts: 1.28 us -> 0 us
  Pallas kernels: 14.3 us -> 14.6 us
    unnamed x1 -> x0, local copies, waits for them, and re-layouts: 1.28 us -> none
    pallas_call x1 -> x2, Pallas kernels: 14.3 us -> 14.6 us  [the longest x1 13.3 us: on_device(): pl.pallas_call(functools.partial(kernel, n_sky, n_tm, span), out_shape=pl...]
where the time goes in v2:
time: 14.8 us; the launch traced here: 14.7 us
  Pallas kernels  14.6 us (99%)
    pallas_call x1, Pallas kernels, on_device(): pl.pallas_call(functools.partial(kernel, n_sky, n_tm, span), out_shape=pl...  13.3 us
    pallas_call x1, Pallas kernels, on_device(): pl.pallas_call(solve_kernel, out_shape=jax.ShapeDtypeStruct(prior.shape,...  1.34 us

profile of v2, /device:TPU:0, one launch (start us, length us, event | category | flops | bytes accessed | tf_op | source)
XLA Modules:
  0.0 14.7 jit_solution(1658440475557990147)
XLA Ops:
  0.0 13.3 %shard_map.91.total_ref = f32[8,128]{1,0:T(8,128)S(1)} custom-call(f32[4,128]{1,0:T(4,128)} %bitcast.13, f32[64,128]{1,0:T(8,128)} %bitcast.8, f32[64,128]{1,0:T(8,128)} %bitcast.9, f32[64,128]{1,0:T(8,128)} %bitcast.10, f32[64,128]{1,0:T(8,128)} %bitcast.11, s32[64,128]{1,0:T(8,128)} %bitcast.12, s32[2,128]{1,0:T(2,128)} %bitcast.14, s32[2,128]{1,0:T(2,128)} %bitcast.15), custom_call_target="tpu_custom_call" | custom-call | tf_op jit(solution)/shard_map/pallas_call | solution.py:240
  13.3 1.3 %shard_map.92 = f32[5,8]{1,0:T(8,128)} custom-call(f32[8,128]{1,0:T(8,128)S(1)} %shard_map.91.total_ref, f32[5,8]{1,0:T(8,128)} %prior_hbm.1), custom_call_target="tpu_custom_call" | custom-call | tf_op jit(solution)/shard_map/pallas_call | solution.py:268

commit v3 on v2

--- a/solution.py
+++ b/solution.py
@@ -50,13 +50,29 @@
     return result
 
 
+def near_peers(tm, n_tm):
+    if n_tm & (n_tm - 1):
+        return [lax.rem(tm + d, n_tm) for d in range(1, n_tm)]
+    bits = [1 << i for i in range(n_tm.bit_length() - 1)]
+    return [tm + bit * (1 - 2 * ((tm // bit) % 2)) for bit in bits]
+
+
+def meet(met, near, step):
+    if step > 0:
+        pl.semaphore_wait(met.at[step - 1], 1)
+    if step < len(near) - 1:
+        pl.semaphore_signal(
+            met.at[step], inc=1, device_id={"tm": near[step + 1]}, device_id_type=MESH
+        )
+
+
 def kernel(
     n_sky, n_tm, span,
     attitude_hbm, time_hbm, parallax_hbm, observed_hbm, phase_hbm, knot_hbm,
-    source_hbm, count_hbm,
-    out_ref,
+    source_hbm, count_hbm, prior_hbm,
+    out_ref, prior_ref,
     table, coef, reals, ints, spread, parts, member, tiles, landed,
-    real_sem, int_sem, att_send, att_recv, sum_send, sum_recv,
+    real_sem, int_sem, prior_sem, own_sem, att_send, att_recv, sum_send, sum_recv, met,
 ):
     sky = lax.axis_index("sky")
     tm = lax.axis_index("tm")
@@ -75,15 +91,17 @@
         pl.semaphore_signal(
             barrier, inc=1, device_id={"sky": lax.rem(sky + d, n_sky)}, device_id_type=MESH
         )
-    for d in range(1, n_tm):
-        pl.semaphore_signal(
-            barrier, inc=1, device_id={"tm": lax.rem(tm + d, n_tm)}, device_id_type=MESH
-        )
-    pltpu.make_async_copy(attitude_hbm, table.at[sky], att_recv).start()
+    near = near_peers(tm, n_tm)
+    for peer in near:
+        pl.semaphore_signal(barrier, inc=1, device_id={"tm": peer}, device_id_type=MESH)
+    own = pltpu.make_async_copy(attitude_hbm, table.at[sky], own_sem)
+    own.start()
     for src, dst in ((source_hbm, source_v), (count_hbm, count_v), (knot_hbm, knot_v)):
         pltpu.make_async_copy(src, dst, int_sem).start()
     for i, src in enumerate((phase_hbm, time_hbm, parallax_hbm, observed_hbm)):
         pltpu.make_async_copy(src, reals.at[i], real_sem).start()
+    prior_copy = pltpu.make_async_copy(prior_hbm, prior_ref, prior_sem)
+    prior_copy.start()
 
     lane_out = lax.broadcasted_iota(jnp.int32, (LANES, LANES), 1)
     lane_in = lax.broadcasted_iota(jnp.int32, (LANES, LANES), 0)
@@ -91,11 +109,12 @@
     for x in range(20):
         spread[x * LANES : (x + 1) * LANES, :] = jnp.where(base == x, 1.0, 0.0).astype(jnp.bfloat16)
 
-    pl.semaphore_wait(barrier, n_sky - 1 + n_tm - 1)
+    own.wait()
+    pl.semaphore_wait(barrier, n_sky - 1 + len(near))
 
     for d in range(1, n_sky):
         pltpu.make_async_remote_copy(
-            src_ref=attitude_hbm,
+            src_ref=table.at[sky],
             dst_ref=table.at[sky],
             send_sem=att_send,
             recv_sem=att_recv,
@@ -103,6 +122,7 @@
             device_id_type=MESH,
         ).start()
 
+    meet(met, near, 0)
     pltpu.make_async_copy(ints, ints, int_sem).wait()
 
     width = 3 * rows
@@ -121,8 +141,11 @@
         hit = jnp.broadcast_to(ids[q : q + 1, :], (sources, width)) == which
         member[q * sources : (q + 1) * sources, :] = jnp.where(hit, 1.0, 0.0).astype(jnp.bfloat16)
 
+    for step in range(1, len(near) - 1):
+        meet(met, near, step)
     pltpu.make_async_copy(reals, reals, real_sem).wait()
-    pltpu.make_async_copy(table, table, att_recv).wait()
+    others = table.at[: n_sky - 1]
+    pltpu.make_async_copy(others, others, att_recv).wait()
 
     per = table.shape[2] // LANES
     chunks = [
@@ -191,6 +214,8 @@
     for q in range(1, segs):
         normal = jnp.where(lane_s == q, by_seg[q * sources : (q + 1) * sources], normal)
     tiles[...] = normal.reshape(n_tm, owned, LANES)
+    if len(near) > 1:
+        pl.semaphore_wait(met.at[len(near) - 2], 1)
 
     for d in range(1, n_tm):
         peer = lax.rem(tm + d, n_tm)
@@ -207,20 +232,17 @@
     for d in range(1, n_tm):
         total = total + landed[d - 1]
     out_ref[...] = total
-    others = table.at[: n_sky - 1]
+    prior_copy.wait()
     pltpu.make_async_copy(others, others, att_send).wait()
     pltpu.make_async_copy(landed, landed, sum_send).wait()
 
 
-def solve_kernel(total_ref, prior_hbm, out_ref, turned, prior_ref, sem):
-    copy = pltpu.make_async_copy(prior_hbm, prior_ref, sem)
-    copy.start()
+def solve_kernel(total_ref, prior_ref, out_ref, turned):
     total = total_ref[...]
     full = total
     for shift in range(ROWS, LANES, ROWS):
         full = full + pltpu.roll(total, shift, 1)
     turned[...] = jnp.transpose(full)
-    copy.wait()
     result = solve_rows(lambda i: turned[i : i + 1, :], lambda i: prior_ref[i : i + 1, :])
     for i in range(5):
         out_ref[i : i + 1, :] = result[i]
@@ -237,11 +259,11 @@
     shape = (rows, LANES)
     vmem = pltpu.VMEM
     f32, i32, bf16 = jnp.float32, jnp.int32, jnp.bfloat16
-    total = pl.pallas_call(
+    total, prior_near = pl.pallas_call(
         functools.partial(kernel, n_sky, n_tm, span),
-        out_shape=pltpu.VMEM((owned, LANES), f32),
-        in_specs=[pl.BlockSpec(memory_space=pl.ANY)] * 8,
-        out_specs=pl.BlockSpec(memory_space=pltpu.VMEM),
+        out_shape=(pltpu.VMEM((owned, LANES), f32), pltpu.VMEM(prior.shape, f32)),
+        in_specs=[pl.BlockSpec(memory_space=pl.ANY)] * 9,
+        out_specs=(pl.BlockSpec(memory_space=pltpu.VMEM),) * 2,
         scratch_shapes=[
             vmem((n_sky, 4, knots), f32),
             vmem((4, n_chunks * 4, LANES), f32),
@@ -253,7 +275,8 @@
             vmem((n_tm, owned, LANES), f32),
             vmem((n_tm - 1, owned, LANES), f32),
         ]
-        + [pltpu.SemaphoreType.DMA] * 6,
+        + [pltpu.SemaphoreType.DMA] * 8
+        + [pltpu.SemaphoreType.REGULAR((max(1, len(near_peers(0, n_tm)) - 1),))],
         compiler_params=pltpu.CompilerParams(collective_id=0, has_side_effects=True),
     )(
         attitude.reshape(4, knots),
@@ -264,13 +287,17 @@
         knot.reshape(shape),
         source.reshape(blocks // LANES, LANES),
         count.reshape(blocks // LANES, LANES),
+        prior,
     )
     return pl.pallas_call(
         solve_kernel,
         out_shape=jax.ShapeDtypeStruct(prior.shape, f32),
-        in_specs=[pl.BlockSpec(memory_space=pltpu.VMEM), pl.BlockSpec(memory_space=pl.ANY)],
-        scratch_shapes=[vmem((LANES, owned), f32), vmem(prior.shape, f32), pltpu.SemaphoreType.DMA],
-    )(pltpu.with_memory_space_constraint(total, pltpu.VMEM), prior)
+        in_specs=[pl.BlockSpec(memory_space=pltpu.VMEM)] * 2,
+        scratch_shapes=[vmem((LANES, owned), f32)],
+    )(
+        pltpu.with_memory_space_constraint(total, pltpu.VMEM),
+        pltpu.with_memory_space_constraint(prior_near, pltpu.VMEM),
+    )
 
 
 def solution(mesh):

time: 14.8 us -> 14.1 us (0.953)
  Pallas kernels: 14.6 us -> 13.9 us
    pallas_call x1, Pallas kernels: 1.34 us -> 0.79 us  [on_device(): pl.pallas_call(solve_kernel, out_shape=jax.ShapeDtypeStruct(prior.shape,...]
    pallas_call x1, Pallas kernels: 13.3 us -> 13.1 us  [on_device(): pl.pallas_call(functools.partial(kernel, n_sky, n_tm, span), out_shape=(p...]
where the time goes in v3:
time: 14.1 us; the launch traced here: 13.9 us
  Pallas kernels  13.9 us (99%)
    pallas_call x1, Pallas kernels, on_device(): pl.pallas_call(functools.partial(kernel, n_sky, n_tm, span), out_shape=(p...  13.1 us
    pallas_call x1, Pallas kernels, on_device(): pl.pallas_call(solve_kernel, out_shape=jax.ShapeDtypeStruct(prior.shape,...  0.79 us

profile of v3, /device:TPU:0, one launch (start us, length us, event | category | flops | bytes accessed | tf_op | source)
XLA Modules:
  0.0 13.9 jit_solution(3520676979636354341)
XLA Ops:
  0.0 13.1 %shard_map.91 = (f32[8,128]{1,0:T(8,128)S(1)}, f32[5,8]{1,0:T(8,128)S(1)}) custom-call(f32[4,128]{1,0:T(4,128)} %bitcast.13, f32[64,128]{1,0:T(8,128)} %bitcast.8, f32[64,128]{1,0:T(8,128)} %bitcast.9, f32[64,128]{1,0:T(8,128)} %bitcast.10, f32[64,128]{1,0:T(8,128)} %bitcast.11, s32[64,128]{1,0:T(8,128)} %bitcast.12, s32[2,128]{1,0:T(2,128)} %bitcast.14, ...), custom_call_target="tpu_custom_call" | custom-call | tf_op jit(solution)/shard_map/pallas_call | solution.py:262
  13.1 0.8 %shard_map.92 = f32[5,8]{1,0:T(8,128)} custom-call(f32[8,128]{1,0:T(8,128)S(1)} %get-tuple-element.7.total_ref, f32[5,8]{1,0:T(8,128)S(1)} %get-tuple-element.8.prior_ref), custom_call_target="tpu_custom_call" | custom-call | tf_op jit(solution)/shard_map/pallas_call | solution.py:292

commit v4 on v3

--- a/solution.py
+++ b/solution.py
@@ -24,6 +24,11 @@
     mid = rest.astype(jnp.bfloat16)
     low = (rest - mid.astype(jnp.float32)).astype(jnp.bfloat16)
     return high, mid, low
+
+
+def split2(value):
+    high = value.astype(jnp.bfloat16)
+    return high, (value - high.astype(jnp.float32)).astype(jnp.bfloat16)
 
 
 def solve_rows(row, prior_row):
@@ -51,19 +56,25 @@
 
 
 def near_peers(tm, n_tm):
-    if n_tm & (n_tm - 1):
-        return [lax.rem(tm + d, n_tm) for d in range(1, n_tm)]
-    bits = [1 << i for i in range(n_tm.bit_length() - 1)]
-    return [tm + bit * (1 - 2 * ((tm // bit) % 2)) for bit in bits]
-
-
-def meet(met, near, step):
-    if step > 0:
-        pl.semaphore_wait(met.at[step - 1], 1)
-    if step < len(near) - 1:
-        pl.semaphore_signal(
-            met.at[step], inc=1, device_id={"tm": near[step + 1]}, device_id_type=MESH
-        )
+    if n_tm % 2 == 0 and n_tm <= 8:
+        edges = [(tm + 1 - 2 * (tm % 2), None), (tm + 2, tm + 2 < n_tm), (tm - 2, tm >= 2)]
+        return edges, n_tm // 2 - 1
+    if n_tm & (n_tm - 1) == 0:
+        bits = [1 << i for i in range(n_tm.bit_length() - 1)]
+        return [(tm + bit * (1 - 2 * ((tm // bit) % 2)), None) for bit in bits], len(bits) - 1
+    return [(lax.rem(tm + d, n_tm), None) for d in range(1, n_tm)], 0
+
+
+def tell(semaphore, edges):
+    for peer, exists in edges:
+
+        def send(peer=peer):
+            pl.semaphore_signal(semaphore, inc=1, device_id={"tm": peer}, device_id_type=MESH)
+
+        if exists is None:
+            send()
+        else:
+            pl.when(exists)(send)
 
 
 def kernel(
@@ -91,9 +102,9 @@
         pl.semaphore_signal(
             barrier, inc=1, device_id={"sky": lax.rem(sky + d, n_sky)}, device_id_type=MESH
         )
-    near = near_peers(tm, n_tm)
-    for peer in near:
-        pl.semaphore_signal(barrier, inc=1, device_id={"tm": peer}, device_id_type=MESH)
+    edges, rounds = near_peers(tm, n_tm)
+    degree = sum(1 if exists is None else exists.astype(jnp.int32) for _, exists in edges)
+    tell(barrier, edges)
     own = pltpu.make_async_copy(attitude_hbm, table.at[sky], own_sem)
     own.start()
     for src, dst in ((source_hbm, source_v), (count_hbm, count_v), (knot_hbm, knot_v)):
@@ -110,7 +121,7 @@
         spread[x * LANES : (x + 1) * LANES, :] = jnp.where(base == x, 1.0, 0.0).astype(jnp.bfloat16)
 
     own.wait()
-    pl.semaphore_wait(barrier, n_sky - 1 + len(near))
+    pl.semaphore_wait(barrier, n_sky - 1 + degree)
 
     for d in range(1, n_sky):
         pltpu.make_async_remote_copy(
@@ -122,7 +133,8 @@
             device_id_type=MESH,
         ).start()
 
-    meet(met, near, 0)
+    if rounds:
+        tell(met.at[0], edges)
     pltpu.make_async_copy(ints, ints, int_sem).wait()
 
     width = 3 * rows
@@ -141,11 +153,16 @@
         hit = jnp.broadcast_to(ids[q : q + 1, :], (sources, width)) == which
         member[q * sources : (q + 1) * sources, :] = jnp.where(hit, 1.0, 0.0).astype(jnp.bfloat16)
 
-    for step in range(1, len(near) - 1):
-        meet(met, near, step)
+    for step in range(1, min(2, rounds)):
+        pl.semaphore_wait(met.at[step - 1], degree)
+        tell(met.at[step], edges)
     pltpu.make_async_copy(reals, reals, real_sem).wait()
     others = table.at[: n_sky - 1]
     pltpu.make_async_copy(others, others, att_recv).wait()
+
+    for step in range(2, rounds):
+        pl.semaphore_wait(met.at[step - 1], degree)
+        tell(met.at[step], edges)
 
     per = table.shape[2] // LANES
     chunks = [
@@ -202,11 +219,11 @@
     for v in range(0, rows // 8, 2):
         first, second = sums_of(v), sums_of(v + 1)
         for x in range(20):
-            for k, part in enumerate(split3(jnp.concatenate([first[x], second[x]], axis=0))):
+            for k, part in enumerate(split2(jnp.concatenate([first[x], second[x]], axis=0))):
                 parts[k * rows + v * 8 : k * rows + v * 8 + 16, x * LANES : (x + 1) * LANES] = part
 
-    three = jnp.dot(parts[...], spread[...], preferred_element_type=jnp.float32)
-    block_sum = three[:rows] + three[rows : 2 * rows] + three[2 * rows :]
+    two = jnp.dot(parts[...], spread[...], preferred_element_type=jnp.float32)
+    block_sum = two[:rows] + two[rows:]
     stacked = jnp.concatenate(split3(block_sum), axis=0)
     by_seg = jnp.dot(member[...], stacked, preferred_element_type=jnp.float32)
     lane_s = lax.broadcasted_iota(jnp.int32, (sources, LANES), 1) // ROWS
@@ -214,8 +231,8 @@
     for q in range(1, segs):
         normal = jnp.where(lane_s == q, by_seg[q * sources : (q + 1) * sources], normal)
     tiles[...] = normal.reshape(n_tm, owned, LANES)
-    if len(near) > 1:
-        pl.semaphore_wait(met.at[len(near) - 2], 1)
+    if rounds:
+        pl.semaphore_wait(met.at[rounds - 1], degree)
 
     for d in range(1, n_tm):
         peer = lax.rem(tm + d, n_tm)
@@ -270,13 +287,13 @@
             vmem((4,) + shape, f32),
             vmem((rows + 2 * (blocks // LANES), LANES), i32),
             vmem((20 * LANES, LANES), bf16),
-            vmem((3 * rows, 20 * LANES), bf16),
+            vmem((2 * rows, 20 * LANES), bf16),
             vmem((segs * sources, 3 * rows), bf16),
             vmem((n_tm, owned, LANES), f32),
             vmem((n_tm - 1, owned, LANES), f32),
         ]
         + [pltpu.SemaphoreType.DMA] * 8
-        + [pltpu.SemaphoreType.REGULAR((max(1, len(near_peers(0, n_tm)) - 1),))],
+        + [pltpu.SemaphoreType.REGULAR((max(1, near_peers(0, n_tm)[1]),))],
         compiler_params=pltpu.CompilerParams(collective_id=0, has_side_effects=True),
     )(
         attitude.reshape(4, knots),

time: 14.1 us -> 14 us (level)
  no operation moved by 1% of the time
where the time goes in v4:
time: 14 us; the launch traced here: 13.8 us
  Pallas kernels  13.8 us (99%)
    pallas_call x1, Pallas kernels, on_device(): pl.pallas_call(functools.partial(kernel, n_sky, n_tm, span), out_shape=(p...  13 us
    pallas_call x1, Pallas kernels, on_device(): pl.pallas_call(solve_kernel, out_shape=jax.ShapeDtypeStruct(prior.shape,...  0.79 us

profile of v4, /device:TPU:0, one launch (start us, length us, event | category | flops | bytes accessed | tf_op | source)
XLA Modules:
  0.0 13.8 jit_solution(18308055473653686817)
XLA Ops:
  0.0 13.0 %shard_map.91 = (f32[8,128]{1,0:T(8,128)S(1)}, f32[5,8]{1,0:T(8,128)S(1)}) custom-call(f32[4,128]{1,0:T(4,128)} %bitcast.13, f32[64,128]{1,0:T(8,128)} %bitcast.8, f32[64,128]{1,0:T(8,128)} %bitcast.9, f32[64,128]{1,0:T(8,128)} %bitcast.10, f32[64,128]{1,0:T(8,128)} %bitcast.11, s32[64,128]{1,0:T(8,128)} %bitcast.12, s32[2,128]{1,0:T(2,128)} %bitcast.14, ...), custom_call_target="tpu_custom_call" | custom-call | tf_op jit(solution)/shard_map/pallas_call | solution.py:279
  13.0 0.8 %shard_map.92 = f32[5,8]{1,0:T(8,128)} custom-call(f32[8,128]{1,0:T(8,128)S(1)} %get-tuple-element.7.total_ref, f32[5,8]{1,0:T(8,128)S(1)} %get-tuple-element.8.prior_ref), custom_call_target="tpu_custom_call" | custom-call | tf_op jit(solution)/shard_map/pallas_call | solution.py:309
